TPU v7x, 128 devices: a whole 4x4x4 slice. The times are simulated.
128 devices in a mesh: data: 1, fsdp: 128 (over z, y, x, core).
Axes of the slice: x: 4, y: 4, z: 4, core: 2. Of those that a mesh axis runs over, the one named last changes fastest.
Arguments:
- hidden: bfloat16 [8192, 640], P('data')
- targets: int32 [8192], P('data')
- w_out: bfloat16 [262144, 640], P('fsdp')
Outputs:
- output 1: float32 [1], P('data')
- output 2: float32 [8192, 640], P(('data', 'fsdp'))
- output 3: float32 [262144, 640], P(('data', 'fsdp'))
All inputs are finite; a program needn't handle non-finite values.
Results may differ from a plain program's by a relative error of at most 0.00115.
Values are sent between devices in bfloat16 or wider.
A program may use at most 1 GiB of HBM per device.

v0:
```python
import jax
import jax.numpy as jnp
from jax import lax
from jax.sharding import PartitionSpec as P


def solution(mesh):
    def local_step(hidden, targets, w_blk):
        tok_group = hidden.shape[0]
        vocab_blk = w_blk.shape[0]
        vocab_start = lax.axis_index("fsdp") * vocab_blk
        logits = jnp.einsum("td,vd->tv", hidden, w_blk, preferred_element_type=jnp.float32)
        row_max = lax.pmax(jnp.max(logits, axis=1, keepdims=True), "fsdp")
        tgt_hit = (lax.broadcasted_iota(jnp.int32, (1, vocab_blk), 1) + vocab_start) == targets[:, None]
        exp_sum = jnp.sum(jnp.exp(logits - row_max), axis=1, keepdims=True)
        tgt_part = jnp.sum(jnp.where(tgt_hit, logits, 0.0), axis=1, keepdims=True)
        group_stats = lax.psum(jnp.concatenate([exp_sum, tgt_part], axis=1), "fsdp")
        log_norm = row_max + jnp.log(group_stats[:, :1])
        loss_val = (jnp.sum(log_norm - group_stats[:, 1:]) / tok_group).reshape(1)
        grad_logits = ((jnp.exp(logits - log_norm) - tgt_hit.astype(jnp.float32)) / tok_group).astype(jnp.bfloat16)
        grad_part = jnp.einsum("tv,vd->td", grad_logits, w_blk, preferred_element_type=jnp.float32)
        grad_hid = lax.psum_scatter(grad_part, "fsdp", scatter_dimension=0, tiled=True)
        grad_w = jnp.einsum("tv,td->vd", grad_logits, hidden, preferred_element_type=jnp.float32)
        return loss_val, grad_hid, grad_w

    return jax.shard_map(
        local_step,
        mesh=mesh,
        in_specs=(P("data", None), P("data"), P("fsdp", None)),
        out_specs=(P("data"), P(("data", "fsdp"), None), P(("data", "fsdp"), None)),
        check_vma=False,
    )
```

profile of v0, /device:TPU:0, one launch (start us, length us, event | category | flops | bytes accessed | tf_op | source)
XLA Modules:
  0.0 1030.6 jit_solution(13646673977945758567)
XLA Ops:
  7.2 0.0 copy-start
  7.2 0.0 all-reduce.2.cloned.1.call-start
  7.2 1.7 copy-done
  8.9 0.0 copy-start.2
  8.9 35.5 %fusion.7 = (f32[8192]{0:T(1024)S(1)}, f32[8192,2048]{0,1:T(8,128)}) fusion(bf16[8192,640]{1,0:T(8,128)(2,1)} %param.3, bf16[2048,640]{1,0:T(8,128)(2,1)S(1)} %copy-done), kind=kOutput, calls=%fused_computation.13 | convolution fusion | flops 21491605504 | bytes 80248832 | tf_op jit(solution)/shard_map/td,vd->tv/dot_general | solution.py:12
  44.4 68.3 %pmax.7 = f32[8192,1]{0,1:T(1,128)S(1)} all-reduce(f32[8192,1]{0,1:T(1,128)S(1)} %bitcast.16), channel_id=1, replica_groups=mesh['data'=1,'fsdp'=128] {'fsdp'}, use_global_device_ids=true, to_apply=%region_1.0 | all-reduce | flops 8192 | bytes 65536 | tf_op jit(solution)/shard_map/pmax | solution.py:13
  112.8 0.0 copy-done.2
  112.8 21.5 %exponential_reduce_fusion = (f32[8192]{0:T(1024)S(1)}, f32[8192]{0:T(1024)S(1)}) fusion(f32[8192,2048]{0,1:T(8,128)} %get-tuple-element.8, f32[8192]{0:T(1024)S(1)} %bitcast.12, s32[8192]{0:T(1024)S(1)} %copy-done.2, s32[2048]{0:T(1024)S(1)} %iota_add_fusion), kind=kLoop, calls=%fused_computation.6 | loop fusion | flops 83869696 | bytes 67248128 | tf_op jit(solution)/shard_map/reduce_sum | solution.py:15
  134.3 0.7 pad_maximum_fusion
  135.0 0.0 all-reduce.2.cloned.1.call-update
  135.0 0.2 reduce-scatter.2.cloned.1.call-start
  135.2 141.2 %all-reduce.2.cloned.1.call-done = f32[8192,2]{0,1:T(2,128)} async-done(((f32[8192,2]{0,1:T(2,128)}), f32[8192,2]{0,1:T(2,128)}) %all-reduce.2.cloned.1.call-update) | async-done | bytes 65552 | tf_op jit(solution)/shard_map/psum | solution.py:17
  276.5 1.6 fusion.5
  278.1 33.3 %fusion.3 = bf16[8192,2048]{0,1:T(8,128)(2,1)} fusion(f32[8192,2048]{0,1:T(8,128)} %get-tuple-element.8, f32[8192]{0:T(1024)S(1)} %bitcast.13, s32[8192]{0:T(1024)S(1)} %copy-done.2, s32[2048]{0:T(1024)S(1)} %iota_add_fusion), kind=kLoop, calls=%fused_computation.5 | loop fusion | flops 100663296 | bytes 100737024 | tf_op jit(solution)/shard_map/convert_element_type | solution.py:20
  311.4 33.0 %fusion.8 = f32[8192,640]{1,0:T(8,128)} fusion(bf16[8192,2048]{0,1:T(8,128)(2,1)} %fusion.3, bf16[2048,640]{1,0:T(8,128)(2,1)S(1)} %copy-done), kind=kOutput, calls=%fused_computation.14 | convolution fusion | flops 21474836480 | bytes 57147392 | tf_op jit(solution)/shard_map/tv,vd->td/dot_general | solution.py:21
  344.3 0.0 reduce-scatter.2.cloned.1.call-update
  345.0 0.0 copy-start.1
  345.0 34.0 %fusion.9 = f32[2048,640]{1,0:T(8,128)} fusion(bf16[8192,2048]{0,1:T(8,128)(2,1)} %fusion.3, bf16[8192,640]{1,0:T(8,128)(2,1)} %param.3), kind=kOutput, calls=%fused_computation.15 | convolution fusion | flops 21474836480 | bytes 49283072 | tf_op jit(solution)/shard_map/tv,td->vd/dot_general | solution.py:23
  379.1 643.5 %reduce-scatter.2.cloned.1.call-done = f32[64,640]{1,0:T(8,128)} async-done(((f32[8192,640]{1,0:T(8,128)}), f32[64,640]{1,0:T(8,128)}) %reduce-scatter.2.cloned.1.call-update) | async-done | bytes 163856 | tf_op jit(solution)/shard_map/reduce_scatter | solution.py:22
  1022.6 0.0 copy-done.1
  (1 shorter events, 0.0 us)
Async XLA Ops:
  7.2 1.8 copy-start
  7.2 269.3 %all-reduce.2.cloned.1.call-start = ((), (), s32[]{:S(2)}) async-start(), calls=%async_computation.1 | async-start | bytes 131072 | tf_op jit(solution)/shard_map/psum | solution.py:17
  8.9 103.9 %copy-start.2 = (s32[8192]{0:T(1024)S(1)}, s32[8192]{0:T(1024)}, u32[]{:S(2)}) copy-start(s32[8192]{0:T(1024)} %param.4) | copy-start | bytes 98308
  135.0 887.6 %reduce-scatter.2.cloned.1.call-start = ((), (), s32[]{:S(2)}) async-start(), calls=%async_computation.2 | async-start | bytes 21135360 | tf_op jit(solution)/shard_map/reduce_scatter | solution.py:22
  345.0 677.6 %copy-start.1 = (bf16[2048,640]{1,0:T(8,128)(2,1)S(1)}, bf16[2048,640]{1,0:T(8,128)(2,1)}, u32[]{:S(2)}) copy-start(bf16[2048,640]{1,0:T(8,128)(2,1)} %param.5) | copy-start | bytes 7864324
Sparse Core Ops, SparseCore 0:
  135.1 141.2 all-reduce.1
  344.5 678.0 reduce-scatter.1
where the time goes:
time: 1030 us
  waiting for transfers between devices  785 us (76%)
  matrix products  103 us (10%)
  blocking collectives  68.3 us (7%)
  other arithmetic  57.1 us (6%)
  between operations  15.9 us (2%)
    reduce_scatter x1, waiting for transfers between devices, local_step(): lax.psum_scatter(grad_part, 'fsdp', scatter_dimension=0, tiled=True)  644 us
    psum x1, waiting for transfers between devices, local_step(): group_stats = lax.psum(jnp.concatenate([exp_sum, tgt_part], axis=1), 'fsdp')  141 us
    pmax x1, blocking collectives, local_step(): row_max = lax.pmax(jnp.max(logits, axis=1, keepdims=True), 'fsdp')  68.3 us
    dot_general x1, matrix products, local_step(): jnp.einsum('td,vd->tv', hidden, w_blk, preferred_element_type=jnp.float32)  35.5 us
    dot_general x1, matrix products, local_step(): jnp.einsum('tv,td->vd', grad_logits, hidden, preferred_element_type=jnp.f...  34 us
    convert_element_type x1, other arithmetic, local_step(): ((jnp.exp(logits - log_norm) - tgt_hit.astype(jnp.float32)) / tok_group)....  33.3 us
    dot_general x1, matrix products, local_step(): jnp.einsum('tv,vd->td', grad_logits, w_blk, preferred_element_type=jnp.fl...  33 us
    reduce_sum x1, other arithmetic, local_step(): exp_sum = jnp.sum(jnp.exp(logits - row_max), axis=1, keepdims=True)  21.5 us
  transfers between devices with their start and end apart: 2, of which 2 were waited for; matrix products, arithmetic and copies ran while one was open for 3% of the time, Pallas kernels for 0%

commit v1 on v0

v1 whole, which is shorter than its diff:
```python
import functools

import jax
import jax.numpy as jnp
from jax import lax
from jax.experimental import pallas as pl
from jax.experimental.pallas import tpu as pltpu
from jax.sharding import PartitionSpec as P

MESH = pl.DeviceIdType.MESH
F32 = jnp.float32
BF16 = jnp.bfloat16

LANES = ((0, 256), (256, 512), (512, 640))
ORDERS = (("x", "y", "z"), ("y", "z", "x"), ("z", "x", "y"))


def remote(src, dst, send, recv, dev):
    return pltpu.make_async_remote_copy(
        src_ref=src, dst_ref=dst, send_sem=send, recv_sem=recv, device_id={"fsdp": dev}, device_id_type=MESH
    )


def greet(peers):
    barrier = pltpu.get_barrier_semaphore()
    for p in peers:
        pl.semaphore_signal(barrier, inc=1, device_id={"fsdp": p}, device_id_type=MESH)
    pl.semaphore_wait(barrier, len(peers))


def merge(parts):
    top = functools.reduce(jnp.maximum, [p[0] for p in parts])
    total = functools.reduce(jnp.add, [p[1] * jnp.exp(p[0] - top) for p in parts])
    target = functools.reduce(jnp.add, [p[2] for p in parts])
    return top, total, target


def stats_kernel(st_ref, out_ref, a_buf, b_buf, o_buf, s1, r1, s2, r2, s3, r3):
    me = lax.axis_index("fsdp")
    g, q = me % 8, me // 8
    row = [q * 8 + (g + k) % 8 for k in range(1, 8)]
    plane = [((q + k) % 16) * 8 + g for k in range(1, 16)]
    greet(row + plane)
    c1 = [remote(st_ref.at[(g + k) % 8], a_buf.at[k - 1], s1.at[k - 1], r1.at[k - 1], row[k - 1]) for k in range(1, 8)]
    for c in c1:
        c.start()
    for c in c1:
        c.wait()
    part = merge([[st_ref[g, i] for i in range(3)]] + [[a_buf[k, i] for i in range(3)] for k in range(7)])
    for i in range(3):
        b_buf[q, i] = part[i]
    c2 = [remote(b_buf.at[q], b_buf.at[q], s2.at[k - 1], r2.at[k - 1], plane[k - 1]) for k in range(1, 16)]
    for c in c2:
        c.start()
    for c in c2:
        c.wait()
    top, total, target = merge([[b_buf[k, i] for i in range(3)] for k in range(16)])
    lse = top + jnp.log(total)
    o_buf[g, 0] = lse
    o_buf[g, 1] = lse - target
    c3 = [remote(o_buf.at[g], o_buf.at[g], s3.at[k - 1], r3.at[k - 1], row[k - 1]) for k in range(1, 8)]
    for c in c3:
        c.start()
    for c in c3:
        c.wait()
    out_ref[...] = o_buf[...]


def stats_exchange(stats):
    dma = pltpu.SemaphoreType.DMA
    return pl.pallas_call(
        stats_kernel,
        out_shape=jax.ShapeDtypeStruct((8, 2, 8, 128), F32),
        in_specs=[pl.BlockSpec(memory_space=pltpu.VMEM)],
        out_specs=pl.BlockSpec(memory_space=pltpu.VMEM),
        scratch_shapes=[
            pltpu.VMEM((7, 3, 8, 128), F32),
            pltpu.VMEM((16, 3, 8, 128), F32),
            pltpu.VMEM((8, 2, 8, 128), F32),
            dma((7,)), dma((7,)), dma((15,)), dma((15,)), dma((7,)), dma((7,)),
        ],
        compiler_params=pltpu.CompilerParams(collective_id=0, has_side_effects=True),
    )(stats)


class Scatter:
    def __init__(self, units, rows, bufs):
        self.units, self.rows = units, rows
        (self.pbuf, self.r0, self.s0, self.v1, self.s1, self.v2, self.s2, self.v3,
         self.csend, self.crecv, self.send, self.recv) = bufs
        me = lax.axis_index("fsdp")
        self.core = me % 2
        self.xyz = {"x": (me // 2) % 4, "y": (me // 8) % 4, "z": me // 32}
        self.me = me
        self.partner = me + 1 - 2 * self.core

    STRIDE = {"x": 2, "y": 8, "z": 32}

    def near(self, axis, k):
        pos = self.xyz[axis]
        return self.me + ((pos + k) % 4 - pos) * self.STRIDE[axis]

    def peers(self):
        return [self.partner] + [self.near(a, k) for a in "xyz" for k in (1, 2, 3)]

    def axes(self, u, j):
        return ORDERS[(j + u) % 3]

    @staticmethod
    def scratch(units, rows, slots):
        dma = pltpu.SemaphoreType.DMA
        widths = [b - a for a, b in LANES]
        return [
            pltpu.VMEM((slots, 64, 2, rows, 640), F32),
            pltpu.VMEM((units, 64, rows, 640), F32),
            [pltpu.VMEM((slots, 2, 4, 8, rows, w), F32) for w in widths],
            [pltpu.VMEM((units, 6, 8, rows, w), F32) for w in widths],
            [pltpu.VMEM((slots, 2, 4, 2, rows, w), F32) for w in widths],
            [pltpu.VMEM((units, 6, 2, rows, w), F32) for w in widths],
            [pltpu.VMEM((slots, 4, rows, w), F32) for w in widths],
            [pltpu.VMEM((units, 3, rows, w), F32) for w in widths],
            dma((units,)), dma((units,)), dma((units, 3, 15)), dma((units, 3, 15)),
        ]

    def core_copy(self, u, slot):
        return remote(self.pbuf.at[slot, :, 1 - self.core], self.r0.at[u], self.csend.at[u], self.crecv.at[u], self.partner)

    def ring_copy(self, u, j, slot, level, kind):
        src, dst = ((self.s0, self.v1), (self.s1, self.v2))[level]
        axis = self.axes(u, j)[level]
        pos = self.xyz[axis]
        up, down = self.near(axis, 1), self.near(axis, 3)
        half, owner, dev = (
            (0, pos + 2, up), (1, pos + 2, down),
            (1, pos + 1, up), (0, pos + 3, down),
            (0, pos + 1, up), (1, pos + 3, down),
        )[kind]
        n = level * 6 + kind
        return remote(src[j].at[slot, half, owner % 4], dst[j].at[u, kind], self.send.at[u, j, n], self.recv.at[u, j, n], dev)

    def last_copy(self, u, j, slot, k):
        axis = self.axes(u, j)[2]
        owner = (self.xyz[axis] + k) % 4
        n = 11 + k
        return remote(self.s2[j].at[slot, owner], self.v3[j].at[u, k - 1], self.send.at[u, j, n], self.recv.at[u, j, n], self.near(axis, k))

    def start_core(self, u, slot):
        self.core_copy(u, slot).start()

    def spread(self, u, slot):
        c = self.core_copy(u, slot)
        c.wait_recv()

        def body(i, _):
            at = {"z": i // 16, "y": (i // 4) % 4, "x": i % 4}
            for j, (lo, hi) in enumerate(LANES):
                a, b, d = (at[n] for n in self.axes(u, j))
                self.s0[j][slot, d // 2, a, b * 2 + d % 2] = (
                    self.pbuf[slot, i, self.core, :, lo:hi] + self.r0[u, i, :, lo:hi]
                )
            return 0

        lax.fori_loop(0, 64, body, 0, unroll=4)
        c.wait_send()
        for kind in range(4):
            for j in range(3):
                self.ring_copy(u, j, slot, 0, kind).start()

    def relay(self, u, slot, level):
        src, dst = ((self.s0, self.v1), (self.s1, self.v2))[level]
        for kind in range(2):
            for j in range(3):
                axis = self.axes(u, j)[level]
                owner = (self.xyz[axis] + (1, 3)[kind]) % 4
                self.ring_copy(u, j, slot, level, kind).wait_recv()
                src[j][slot, kind, owner] = src[j][slot, kind, owner] + dst[j][u, kind]
                self.ring_copy(u, j, slot, level, 4 + kind).start()

    def settle(self, u, slot, level):
        src, dst = ((self.s0, self.v1), (self.s1, self.v2))[level]
        for j in range(3):
            pos = self.xyz[self.axes(u, j)[level]]
            for kind in range(2, 6):
                self.ring_copy(u, j, slot, level, kind).wait_recv()
            for half in range(2):
                total = (src[j][slot, half, pos] + dst[j][u, 4 + half]) + dst[j][u, 3 - half]
                if level == 0:
                    for b in range(4):
                        self.s1[j][slot, half, b] = total[b * 2 : b * 2 + 2]
                else:
                    self.s2[j][slot, half * 2 : half * 2 + 2] = total
            if level == 0:
                for kind in range(4):
                    self.ring_copy(u, j, slot, 1, kind).start()
            else:
                for k in range(1, 4):
                    self.last_copy(u, j, slot, k).start()
        for j in range(3):
            for kind in range(6):
                self.ring_copy(u, j, slot, level, kind).wait_send()

    def finish(self, u, slot, out_ref):
        for j, (lo, hi) in enumerate(LANES):
            for k in range(1, 4):
                self.last_copy(u, j, slot, k).wait_recv()
            pos = self.xyz[self.axes(u, j)[2]]
            total = (self.s2[j][slot, pos] + self.v3[j][u, 0]) + (self.v3[j][u, 1] + self.v3[j][u, 2])
            out_ref[u * self.rows : (u + 1) * self.rows, lo:hi] = total
        for j in range(3):
            for k in range(1, 4):
                self.last_copy(u, j, slot, k).wait_send()


UNITS, ROWS, SLOTS = 4, 16, 2


def scatter_kernel(part_ref, out_ref, load_sem, *bufs):
    rs = Scatter(UNITS, ROWS, bufs)
    greet(rs.peers())

    def load(u):
        return pltpu.make_async_copy(part_ref.at[:, :, u], rs.pbuf.at[u % SLOTS], load_sem.at[u])

    stages = [
        lambda u, s: load(u).start(),
        lambda u, s: (load(u).wait(), rs.start_core(u, s)),
        rs.spread,
        lambda u, s: rs.relay(u, s, 0),
        lambda u, s: rs.settle(u, s, 0),
        lambda u, s: rs.relay(u, s, 1),
        lambda u, s: rs.settle(u, s, 1),
        lambda u, s: rs.finish(u, s, out_ref),
    ]
    for t in range(UNITS + len(stages) - 1):
        for n in reversed(range(len(stages))):
            if 0 <= t - n < UNITS:
                stages[n](t - n, (t - n) % SLOTS)


def scatter(part):
    return pl.pallas_call(
        scatter_kernel,
        out_shape=jax.ShapeDtypeStruct((64, 640), F32),
        in_specs=[pl.BlockSpec(memory_space=pl.ANY)],
        out_specs=pl.BlockSpec(memory_space=pltpu.VMEM),
        scratch_shapes=[pltpu.SemaphoreType.DMA((UNITS,))] + Scatter.scratch(UNITS, ROWS, SLOTS),
        compiler_params=pltpu.CompilerParams(collective_id=1, has_side_effects=True, vmem_limit_bytes=60 * 2**20),
    )(part.reshape(64, 2, UNITS, ROWS, 640))


def solution(mesh):
    def local_step(hidden, targets, w_blk):
        tokens, vocab = hidden.shape[0], w_blk.shape[0]
        start = lax.axis_index("fsdp") * vocab
        logits = jnp.einsum("td,vd->tv", hidden, w_blk, preferred_element_type=F32)
        top = jnp.max(logits, axis=1, keepdims=True)
        hit = (lax.broadcasted_iota(jnp.int32, (1, vocab), 1) + start) == targets[:, None]
        total = jnp.sum(jnp.exp(logits - top), axis=1)
        target = jnp.sum(jnp.where(hit, logits, 0.0), axis=1)
        stats = jnp.stack([top[:, 0], total, target]).reshape(3, 8, 8, 128).transpose(1, 0, 2, 3)
        got = stats_exchange(stats)
        lse = got[:, 0].reshape(tokens, 1)
        loss = (jnp.sum(got[:, 1]) / tokens).reshape(1)
        dz = ((jnp.exp(logits - lse) - hit.astype(F32)) / tokens).astype(BF16)
        part = jnp.einsum("tv,vd->td", dz, w_blk, preferred_element_type=F32)
        grad_hid = scatter(part)
        grad_w = jnp.einsum("tv,td->vd", dz, hidden, preferred_element_type=F32)
        return loss, grad_hid, grad_w

    return jax.shard_map(
        local_step,
        mesh=mesh,
        in_specs=(P("data", None), P("data"), P("fsdp", None)),
        out_specs=(P("data"), P(("data", "fsdp"), None), P(("data", "fsdp"), None)),
        check_vma=False,
    )
```

time: 1030 us -> 255 us (0.25)
  waiting for transfers between devices: 785 us -> 0 us
  Pallas kernels: 0 us -> 89.8 us
  blocking collectives: 68.3 us -> 0 us
  between operations: 15.9 us -> 2.46 us
    reduce_scatter x1 -> x0, waiting for transfers between devices: 644 us -> none  [local_step(): lax.psum_scatter(grad_part, 'fsdp', scatter_dimension=0, tiled=True)]
    psum x1 -> x0, waiting for transfers between devices: 141 us -> none  [local_step(): group_stats = lax.psum(jnp.concatenate([exp_sum, tgt_part], axis=1), 'fsdp')]
    pallas_call x0 -> x2, Pallas kernels: none -> 89.8 us  [the longest x1 68.1 us: scatter(): pl.pallas_call(scatter_kernel, out_shape=jax.ShapeDtypeStruct((64, 640),...]
    pmax x1 -> x0, blocking collectives: 68.3 us -> none  [local_step(): row_max = lax.pmax(jnp.max(logits, axis=1, keepdims=True), 'fsdp')]
    reduce_sum x2 -> x1, other arithmetic: 23.1 us -> 21.5 us  [local_step(): total = jnp.sum(jnp.exp(logits - top), axis=1)]
  transfers between devices with their start and end apart: 2 -> 0, of which waited for: 2 -> 0; matrix products, arithmetic and copies ran while one was open for 3% -> 0% of each run, Pallas kernels for 0% -> 0%
where the time goes in v1:
time: 255 us
  matrix products  102 us (40%)
  Pallas kernels  89.8 us (35%)
  other arithmetic  56.9 us (22%)
  local copies, waits for them, and re-layouts  3.32 us (1%)
    pallas_call x1, Pallas kernels, scatter(): pl.pallas_call(scatter_kernel, out_shape=jax.ShapeDtypeStruct((64, 640),...  68.1 us
    dot_general x1, matrix products, local_step(): logits = jnp.einsum('td,vd->tv', hidden, w_blk, preferred_element_type=F32)  35.5 us
    dot_general x1, matrix products, local_step(): grad_w = jnp.einsum('tv,td->vd', dz, hidden, preferred_element_type=F32)  33.7 us
    convert_element_type x1, other arithmetic, local_step(): dz = ((jnp.exp(logits - lse) - hit.astype(F32)) / tokens).astype(BF16)  33.3 us
    dot_general x1, matrix products, local_step(): part = jnp.einsum('tv,vd->td', dz, w_blk, preferred_element_type=F32)  33 us
    pallas_call x1, Pallas kernels, stats_exchange(): pl.pallas_call(stats_kernel, out_shape=jax.ShapeDtypeStruct((8, 2, 8, 128...  21.7 us
    reduce_sum x1, other arithmetic, local_step(): total = jnp.sum(jnp.exp(logits - top), axis=1)  21.5 us

profile of v1, /device:TPU:0, one launch (start us, length us, event | category | flops | bytes accessed | tf_op | source)
XLA Modules:
  0.0 254.6 jit_solution(11304921896808502624)
XLA Ops:
  0.6 0.0 copy-start
  0.7 1.7 copy-done
  2.4 0.0 copy-start.1
  2.4 35.5 %fusion.4 = (f32[8192]{0:T(1024)S(1)}, f32[8192,2048]{0,1:T(8,128)}) fusion(bf16[8192,640]{1,0:T(8,128)(2,1)} %param.3, bf16[2048,640]{1,0:T(8,128)(2,1)S(1)} %copy-done), kind=kOutput, calls=%fused_computation.11 | convolution fusion | flops 21491605504 | bytes 80248832 | tf_op jit(solution)/shard_map/td,vd->tv/dot_general | solution.py:255
  37.9 0.0 copy-done.1
  37.9 21.5 %exponential_reduce_fusion = (f32[8192]{0:T(1024)S(1)}, f32[8192]{0:T(1024)S(1)}) fusion(f32[8192,2048]{0,1:T(8,128)} %get-tuple-element.8, f32[8192]{0:T(1024)S(1)} %get-tuple-element.7, s32[8192]{0:T(1024)S(1)} %copy-done.1, s32[2048]{0:T(1024)S(1)} %iota_add_fusion), kind=kLoop, calls=%fused_computation.6 | loop fusion | flops 83869696 | bytes 67248128 | tf_op jit(solution)/shard_map/reduce_sum | solution.py:258
  59.4 0.6 maximum_bitcast_fusion.st_ref
  60.0 21.7 %shard_map.58 = f32[8,2,8,128]{3,2,1,0:T(8,128)} custom-call(f32[8,3,8,128]{3,2,1,0:T(8,128)} %maximum_bitcast_fusion.st_ref), custom_call_target="tpu_custom_call" | custom-call | tf_op jit(solution)/shard_map/pallas_call | solution.py:71
  81.7 1.4 slice_bitcast_fusion
  83.7 33.3 %fusion.3 = bf16[8192,2048]{0,1:T(8,128)(2,1)} fusion(f32[8192,2048]{0,1:T(8,128)} %get-tuple-element.8, f32[8192]{0:T(1024)S(1)} %get-tuple-element.5, s32[8192]{0:T(1024)S(1)} %copy-done.1, s32[2048]{0:T(1024)S(1)} %iota_add_fusion), kind=kLoop, calls=%fused_computation.5 | loop fusion | flops 100663296 | bytes 100737024 | tf_op jit(solution)/shard_map/convert_element_type | solution.py:264
  117.1 33.7 %fusion.6 = f32[2048,640]{1,0:T(8,128)} fusion(bf16[8192,2048]{0,1:T(8,128)(2,1)} %fusion.3, bf16[8192,640]{1,0:T(8,128)(2,1)} %param.3), kind=kOutput, calls=%fused_computation.13 | convolution fusion | flops 21474836480 | bytes 49283072 | tf_op jit(solution)/shard_map/tv,td->vd/dot_general | solution.py:267
  150.7 33.0 %fusion.5 = f32[8192,640]{1,0:T(8,128)} fusion(bf16[8192,2048]{0,1:T(8,128)(2,1)} %fusion.3, bf16[2048,640]{1,0:T(8,128)(2,1)S(1)} %copy-done), kind=kOutput, calls=%fused_computation.12 | convolution fusion | flops 21474836480 | bytes 57147392 | tf_op jit(solution)/shard_map/tv,vd->td/dot_general | solution.py:265
  183.7 68.1 %shard_map.59 = f32[64,640]{1,0:T(8,128)} custom-call(f32[64,2,4,16,640]{4,3,2,1,0:T(8,128)} %bitcast.15), custom_call_target="tpu_custom_call" | custom-call | tf_op jit(solution)/shard_map/pallas_call | solution.py:241
  251.9 1.6 copy.7
  (1 shorter events, 0.0 us)
Async XLA Ops:
  0.6 1.7 copy-start
  2.4 35.5 %copy-start.1 = (s32[8192]{0:T(1024)S(1)}, s32[8192]{0:T(1024)}, u32[]{:S(2)}) copy-start(s32[8192]{0:T(1024)} %param.4) | copy-start | bytes 98308

commit v2 on v0

v2 whole, which is shorter than its diff:
```python
import functools

import jax
import jax.numpy as jnp
from jax import lax
from jax.experimental import pallas as pl
from jax.experimental.pallas import tpu as pltpu
from jax.sharding import PartitionSpec as P

MESH = pl.DeviceIdType.MESH
F32 = jnp.float32
BF16 = jnp.bfloat16
COMM = True

TOKENS, DIM, VOCAB = 8192, 640, 2048
UNITS, ROWS = 8, 8
SIZE = TOKENS // UNITS
BLOCK = 256
SLOTS = 4
LANES = ((0, 256), (256, 512), (512, 640))
STRIDES = (2, 8, 32)


def dot(a, b, ca, cb):
    return lax.dot_general(a, b, (((ca,), (cb,)), ((), ())), preferred_element_type=F32)


def pick(n, values):
    return jnp.where(n == 0, values[0], jnp.where(n == 1, values[1], values[2]))


def remote(src, dst, send, recv, dev):
    return pltpu.make_async_remote_copy(
        src_ref=src, dst_ref=dst, send_sem=send, recv_sem=recv, device_id={"fsdp": dev}, device_id_type=MESH
    )


def merge(parts):
    top = functools.reduce(jnp.maximum, [p[0:1] for p in parts])
    total = functools.reduce(jnp.add, [p[1:2] * jnp.exp(p[0:1] - top) for p in parts])
    return top, total


class Place:
    def __init__(self):
        self.me = me = lax.axis_index("fsdp") if COMM else 5
        self.g, self.q = me % 8, me // 8
        self.core = me % 2
        self.partner = me + 1 - 2 * self.core
        self.pos = ((me // 2) % 4, (me // 8) % 4, me // 32)
        self.row = [self.q * 8 + (self.g + k) % 8 for k in range(1, 8)]
        self.plane = [((self.q + k) % 16) * 8 + self.g for k in range(1, 16)]

    def near(self, axis, k):
        pos = pick(axis, self.pos)
        return self.me + ((pos + k) % 4 - pos) * pick(axis, STRIDES)

    def greet(self):
        barrier = pltpu.get_barrier_semaphore()
        for p in self.row + self.plane:
            pl.semaphore_signal(barrier, inc=1, device_id={"fsdp": p}, device_id_type=MESH)
        pl.semaphore_wait(barrier, 22)


class Stats:
    def __init__(self, place, bufs):
        self.p = place
        self.own, self.a, self.b, self.lse, self.send, self.recv = bufs

    @staticmethod
    def scratch():
        dma = pltpu.SemaphoreType.DMA
        return [
            pltpu.VMEM((SLOTS, 8, 2, 128), F32),
            pltpu.VMEM((SLOTS, 7, 2, 128), F32),
            pltpu.VMEM((SLOTS, 16, 2, 128), F32),
            pltpu.VMEM((SLOTS, 8, 1, 128), F32),
            dma((SLOTS, 29)),
            dma((SLOTS, 29)),
        ]

    def first(self, s):
        return [
            remote(self.own.at[s, (self.p.g + k) % 8], self.a.at[s, k - 1], self.send.at[s, k - 1], self.recv.at[s, k - 1], self.p.row[k - 1])
            for k in range(1, 8)
        ]

    def second(self, s):
        mine = self.b.at[s, self.p.q]
        return [
            remote(mine, mine, self.send.at[s, 6 + k], self.recv.at[s, 6 + k], self.p.plane[k - 1])
            for k in range(1, 16)
        ]

    def third(self, s):
        mine = self.lse.at[s, self.p.g]
        return [
            remote(mine, mine, self.send.at[s, 21 + k], self.recv.at[s, 21 + k], self.p.row[k - 1])
            for k in range(1, 8)
        ]

    def start_first(self, s):
        for c in self.first(s):
            c.start()

    def start_second(self, s):
        for c in self.first(s):
            c.wait()
        top, total = merge([self.own[s, self.p.g]] + [self.a[s, k] for k in range(7)])
        self.b[s, self.p.q] = jnp.concatenate([top, total], axis=0)
        for c in self.second(s):
            c.start()

    def start_third(self, s):
        for c in self.second(s):
            c.wait()
        top, total = merge([self.b[s, k] for k in range(16)])
        self.lse[s, self.p.g] = top + jnp.log(total)
        for c in self.third(s):
            c.start()

    def wait_third(self, s):
        for c in self.third(s):
            c.wait()


class Scatter:
    def __init__(self, place, bufs):
        self.p = place
        (self.pbuf, self.r0, self.s0, self.v1, self.s1, self.v2, self.s2, self.v3,
         self.csend, self.crecv, self.send, self.recv) = bufs

    @staticmethod
    def scratch():
        dma = pltpu.SemaphoreType.DMA
        widths = [b - a for a, b in LANES]
        return [
            pltpu.VMEM((64, 2, ROWS, DIM), F32),
            pltpu.VMEM((2, 64, ROWS, DIM), F32),
            [pltpu.VMEM((2, 2, 4, 8, ROWS, w), F32) for w in widths],
            [pltpu.VMEM((SLOTS, 6, 8, ROWS, w), F32) for w in widths],
            [pltpu.VMEM((2, 2, 4, 2, ROWS, w), F32) for w in widths],
            [pltpu.VMEM((SLOTS, 6, 2, ROWS, w), F32) for w in widths],
            [pltpu.VMEM((2, 4, ROWS, w), F32) for w in widths],
            [pltpu.VMEM((SLOTS, 3, ROWS, w), F32) for w in widths],
            dma((2,)), dma((2,)), dma((SLOTS, 3, 15)), dma((SLOTS, 3, 15)),
        ]

    def axis(self, u, j, level):
        return (u + j + level) % 3

    def bufs(self, level):
        return ((self.s0, self.v1), (self.s1, self.v2))[level]

    def core_copy(self, u):
        s = u % 2
        return remote(self.pbuf.at[:, 1 - self.p.core], self.r0.at[s], self.csend.at[s], self.crecv.at[s], self.p.partner)

    def ring_copy(self, u, j, level, kind):
        src, dst = self.bufs(level)
        axis = self.axis(u, j, level)
        pos = pick(axis, self.p.pos)
        half, step, way = ((0, 2, 1), (1, 2, 3), (1, 1, 1), (0, 3, 3), (0, 1, 1), (1, 3, 3))[kind]
        n, s = level * 6 + kind, u % SLOTS
        return remote(
            src[j].at[u % 2, half, (pos + step) % 4], dst[j].at[s, kind], self.send.at[s, j, n], self.recv.at[s, j, n],
            self.p.near(axis, way),
        )

    def last_copy(self, u, j, k):
        axis = self.axis(u, j, 2)
        owner = (pick(axis, self.p.pos) + k) % 4
        n, s = 11 + k, u % SLOTS
        return remote(
            self.s2[j].at[u % 2, owner], self.v3[j].at[s, k - 1], self.send.at[s, j, n], self.recv.at[s, j, n],
            self.p.near(axis, k),
        )

    def start_core(self, u):
        self.core_copy(u).start()

    def spread(self, u):
        c = self.core_copy(u)
        c.wait_recv()
        s = u % 2

        def body(i, _):
            at = (i % 4, (i // 4) % 4, i // 16)
            for j, (lo, hi) in enumerate(LANES):
                a, b, d = (pick(self.axis(u, j, n), at) for n in range(3))
                self.s0[j][s, d // 2, a, b * 2 + d % 2] = (
                    self.pbuf[i, self.p.core, :, lo:hi] + self.r0[s, i, :, lo:hi]
                )
            return 0

        lax.fori_loop(0, 64, body, 0, unroll=4)
        c.wait_send()
        for kind in range(4):
            for j in range(3):
                self.ring_copy(u, j, 0, kind).start()

    def relay(self, u, level):
        src, dst = self.bufs(level)
        for kind in range(2):
            for j in range(3):
                owner = (pick(self.axis(u, j, level), self.p.pos) + (1, 3)[kind]) % 4
                self.ring_copy(u, j, level, kind).wait_recv()
                src[j][u % 2, kind, owner] = src[j][u % 2, kind, owner] + dst[j][u % SLOTS, kind]
                self.ring_copy(u, j, level, 4 + kind).start()

    def settle(self, u, level):
        src, dst = self.bufs(level)
        s, v = u % 2, u % SLOTS
        for j in range(3):
            pos = pick(self.axis(u, j, level), self.p.pos)
            for kind in range(2, 6):
                self.ring_copy(u, j, level, kind).wait_recv()
            for half in range(2):
                total = (src[j][s, half, pos] + dst[j][v, 4 + half]) + dst[j][v, 3 - half]
                if level == 0:
                    for b in range(4):
                        self.s1[j][s, half, b] = total[b * 2 : b * 2 + 2]
                else:
                    self.s2[j][s, half * 2 : half * 2 + 2] = total
            if level == 0:
                for kind in range(4):
                    self.ring_copy(u, j, 1, kind).start()
            else:
                for k in range(1, 4):
                    self.last_copy(u, j, k).start()
        for j in range(3):
            for kind in range(6):
                self.ring_copy(u, j, level, kind).wait_send()

    def finish(self, u, out_ref):
        v = u % SLOTS
        for j, (lo, hi) in enumerate(LANES):
            for k in range(1, 4):
                self.last_copy(u, j, k).wait_recv()
            pos = pick(self.axis(u, j, 2), self.p.pos)
            total = (self.s2[j][u % 2, pos] + self.v3[j][v, 0]) + (self.v3[j][v, 1] + self.v3[j][v, 2])
            out_ref[pl.ds(pl.multiple_of(u * ROWS, ROWS), ROWS), lo:hi] = total
        for j in range(3):
            for k in range(1, 4):
                self.last_copy(u, j, k).wait_send()


def main_kernel(h_ref, w_ref, tgt_ref, loss_ref, dh_ref, dw_ref, hb, wb, zb, dzb, acc, lse_col, tgt_col, lost,
                la, lb, h_sem, w_sem, out_sem, lsend, lrecv, *bufs):
    place = Place()
    stats = Stats(place, bufs[:6])
    rs = Scatter(place, bufs[6:])
    start = place.me * VOCAB

    def load_h(t):
        s = t % 4
        return pltpu.make_async_copy(h_ref.at[:, t], hb.at[s], h_sem.at[s])

    load_w = pltpu.make_async_copy(w_ref, wb, w_sem)
    load_w.start()
    load_h(0).start()
    acc[...] = jnp.zeros_like(acc)
    lost[...] = jnp.zeros_like(lost)
    if COMM:
        place.greet()
    load_w.wait()

    lane = lax.broadcasted_iota(jnp.int32, (64, 128), 1)

    def local_stats(t, rb):
        z, s = t % 3, t % SLOTS
        for half in range(2):
            cols = []
            for part in range(2):
                r = rb * BLOCK + half * 128 + part * 64
                rows = slice(r, r + 64)
                top = functools.reduce(jnp.maximum, [zb[z, rows, c : c + 128] for c in range(0, VOCAB, 128)])
                top = jnp.max(top, axis=1, keepdims=True)
                total = functools.reduce(jnp.add, [jnp.exp(zb[z, rows, c : c + 128] - top) for c in range(0, VOCAB, 128)])
                total = jnp.sum(total, axis=1, keepdims=True)
                cols.append(jnp.where(lane == 0, top, total))
            packed = jnp.concatenate(cols, axis=0).T
            stats.own[s, rb * 2 + half] = packed[0:2]

    def logits(t):
        h = hb.at[t % 4]
        for rb in range(SIZE // BLOCK):
            rows = slice(rb * BLOCK, (rb + 1) * BLOCK)
            d = BLOCK // ROWS
            hv = h[rb * d : (rb + 1) * d].reshape(BLOCK, DIM)
            zb[t % 3, rows, :] = dot(hv, wb[...], 1, 1)
            if rb:
                local_stats(t, rb - 1)
        local_stats(t, SIZE // BLOCK - 1)

    def columns(u):
        for g in range(8):
            rows = slice(g * 128, (g + 1) * 128)
            lse_col[rows, :] = jnp.broadcast_to(stats.lse[u % SLOTS, g], (128, 128)).T
            tgt_col[rows, :] = jnp.broadcast_to(tgt_ref[u, g : g + 1, :] - start, (128, 128)).T

    def grad_logits(u, rb):
        z = u % 3
        for part in range(BLOCK // 64):
            r = rb * BLOCK + part * 64
            rows = slice(r, r + 64)
            lse, tgt = lse_col[rows, :], tgt_col[rows, :]
            found = []
            for c in range(0, VOCAB, 128):
                x = zb[z, rows, c : c + 128] - lse
                hit = (lane + c) == tgt
                found.append(jnp.where(hit, x, 0.0))
                dzb[rows, c : c + 128] = ((jnp.exp(x) - jnp.where(hit, 1.0, 0.0)) * (1.0 / TOKENS)).astype(BF16)
            lost[...] += functools.reduce(jnp.add, found)

    def grad_hidden(u):
        n = SIZE // BLOCK
        d = BLOCK // ROWS // 2
        grad_logits(u, 0)
        for rb in range(n):
            rows = slice(rb * BLOCK, (rb + 1) * BLOCK)
            rs.pbuf[rb * d : (rb + 1) * d] = dot(dzb[rows, :], wb[...], 1, 0).reshape(d, 2, ROWS, DIM)
            if rb + 1 < n:
                grad_logits(u, rb + 1)

    def grad_weight(u):
        acc[...] += dot(hb[u % 4].reshape(SIZE, DIM), dzb[...], 0, 0)

    def step(t, _):
        u = t - 2
        old, older = t - 3, t - 4

        @pl.when(t + 1 < UNITS)
        def _():
            load_h(t + 1).start()

        @pl.when(t < UNITS)
        def _():
            load_h(t).wait()
            logits(t)
            if COMM:
                stats.start_first(t % SLOTS)

        if COMM:
            @pl.when(old >= 0)
            def _():
                rs.relay(old, 0)

            @pl.when(older >= 0)
            def _():
                rs.settle(older, 1)

        @pl.when(u >= 0)
        def _():
            if COMM:
                stats.wait_third(u % SLOTS)
            columns(u)
            grad_hidden(u)
            if COMM:
                rs.start_core(u)

        if COMM:
            @pl.when((t >= 1) & (t <= UNITS))
            def _():
                stats.start_third((t - 1) % SLOTS)

            @pl.when(old >= 0)
            def _():
                rs.settle(old, 0)

            @pl.when(older >= 0)
            def _():
                rs.finish(older, dh_ref)

        @pl.when(u >= 0)
        def _():
            grad_weight(u)

        if COMM:
            @pl.when(old >= 0)
            def _():
                rs.relay(old, 1)

            @pl.when(u >= 0)
            def _():
                rs.spread(u)

            @pl.when(t < UNITS)
            def _():
                stats.start_second(t % SLOTS)

        return 0

    lax.fori_loop(0, UNITS + 2, step, 0)
    out = pltpu.make_async_copy(acc, dw_ref, out_sem)
    out.start()
    mine = jnp.sum(lost[...], axis=0, keepdims=True)
    if not COMM:
        loss_ref[...] = mine
        out.wait()
        return
    last = UNITS - 1
    la[place.g] = mine
    row = [remote(la.at[place.g], la.at[place.g], lsend.at[k - 1], lrecv.at[k - 1], place.row[k - 1]) for k in range(1, 8)]
    plane = [remote(lb.at[place.q], lb.at[place.q], lsend.at[6 + k], lrecv.at[6 + k], place.plane[k - 1]) for k in range(1, 16)]
    for c in row:
        c.start()
    rs.relay(last, 0)
    rs.settle(last - 1, 1)
    rs.settle(last, 0)
    for c in row:
        c.wait()
    lb[place.q] = functools.reduce(jnp.add, [la[k] for k in range(8)])
    for c in plane:
        c.start()
    rs.finish(last - 1, dh_ref)
    rs.relay(last, 1)
    rs.settle(last, 1)
    for c in plane:
        c.wait()
    loss_ref[...] = functools.reduce(jnp.add, [lb[k] for k in range(16)])
    rs.finish(last, dh_ref)
    out.wait()


def fused(hidden, targets, w_blk):
    dma = pltpu.SemaphoreType.DMA
    any_spec, vmem = pl.BlockSpec(memory_space=pl.ANY), pl.BlockSpec(memory_space=pltpu.VMEM)
    return pl.pallas_call(
        main_kernel,
        out_shape=(
            jax.ShapeDtypeStruct((1, 128), F32),
            jax.ShapeDtypeStruct((64, DIM), F32),
            jax.ShapeDtypeStruct((DIM, VOCAB), F32),
        ),
        in_specs=[any_spec, any_spec, vmem],
        out_specs=(vmem, vmem, any_spec),
        scratch_shapes=[
            pltpu.VMEM((4, 128, ROWS, DIM), BF16),
            pltpu.VMEM((VOCAB, DIM), BF16),
            pltpu.VMEM((3, SIZE, VOCAB), F32),
            pltpu.VMEM((SIZE, VOCAB), BF16),
            pltpu.VMEM((DIM, VOCAB), F32),
            pltpu.VMEM((SIZE, 128), F32),
            pltpu.VMEM((SIZE, 128), jnp.int32),
            pltpu.VMEM((64, 128), F32),
            pltpu.VMEM((8, 1, 128), F32),
            pltpu.VMEM((16, 1, 128), F32),
            dma((4,)), dma, dma, dma((22,)), dma((22,)),
        ] + Stats.scratch() + Scatter.scratch(),
        compiler_params=pltpu.CompilerParams(
            vmem_limit_bytes=67043328, **(dict(collective_id=0, has_side_effects=True) if COMM else {})
        ),
    )(hidden, w_blk, targets)


def prepare(hidden, targets):
    h = hidden.reshape(128, UNITS, ROWS, DIM)
    t = targets.reshape(128, UNITS, ROWS).transpose(1, 0, 2).reshape(UNITS, 8, 128)
    return h, t


def solution(mesh):
    def local_step(hidden, targets, w_blk):
        h, t = prepare(hidden, targets)
        lost, grad_hid, grad_w = fused(h, t, w_blk)
        loss = (-jnp.sum(lost) / hidden.shape[0]).reshape(1)
        return loss, grad_hid, grad_w.T

    return jax.shard_map(
        local_step,
        mesh=mesh,
        in_specs=(P("data", None), P("data"), P("fsdp", None)),
        out_specs=(P("data"), P(("data", "fsdp"), None), P(("data", "fsdp"), None)),
        check_vma=False,
    )
```

time: 1030 us -> 185 us (0.18)
  waiting for transfers between devices: 785 us -> 0 us
  Pallas kernels: 0 us -> 173 us
  matrix products: 103 us -> 0 us
  blocking collectives: 68.3 us -> 0 us
  other arithmetic: 57.1 us -> 1.22 us
  between operations: 15.9 us -> 2.45 us
    reduce_scatter x1 -> x0, waiting for transfers between devices: 644 us -> none  [local_step(): lax.psum_scatter(grad_part, 'fsdp', scatter_dimension=0, tiled=True)]
    pallas_call x0 -> x1, Pallas kernels: none -> 173 us  [fused(): pl.pallas_call(main_kernel, out_shape=(jax.ShapeDtypeStruct((1, 128), F32...]
    psum x1 -> x0, waiting for transfers between devices: 141 us -> none  [local_step(): group_stats = lax.psum(jnp.concatenate([exp_sum, tgt_part], axis=1), 'fsdp')]
    dot_general x3 -> x0, matrix products: 103 us -> none  [the longest x1 35.5 us: local_step(): jnp.einsum('td,vd->tv', hidden, w_blk, preferred_element_type=jnp.float32)]
    pmax x1 -> x0, blocking collectives: 68.3 us -> none  [local_step(): row_max = lax.pmax(jnp.max(logits, axis=1, keepdims=True), 'fsdp')]
    convert_element_type x1 -> x0, other arithmetic: 33.3 us -> none  [local_step(): ((jnp.exp(logits - log_norm) - tgt_hit.astype(jnp.float32)) / tok_group)....]
    reduce_sum x2 -> x1, other arithmetic: 23.1 us -> 1.22 us  [local_step(): loss = (-jnp.sum(lost) / hidden.shape[0]).reshape(1)]
  transfers between devices with their start and end apart: 2 -> 0, of which waited for: 2 -> 0; matrix products, arithmetic and copies ran while one was open for 3% -> 0% of each run, Pallas kernels for 0% -> 0%
where the time goes in v2:
time: 185 us
  Pallas kernels  173 us (94%)
  local copies, waits for them, and re-layouts  8.59 us (5%)
  between operations  2.45 us (1%)
    pallas_call x1, Pallas kernels, fused(): pl.pallas_call(main_kernel, out_shape=(jax.ShapeDtypeStruct((1, 128), F32...  173 us
    unnamed x4, local copies, waits for them, and re-layouts  6.59 us

profile of v2, /device:TPU:0, one launch (start us, length us, event | category | flops | bytes accessed | tf_op | source)
XLA Modules:
  0.0 185.1 jit_solution(2723886914564564126)
XLA Ops:
  0.6 1.0 reshape.19
  1.7 0.1 copy.7
  1.8 0.8 reshape.20.tgt_ref
  2.6 172.8 %shard_map.58 = (f32[1,128]{1,0:T(1,128)}, f32[64,640]{1,0:T(8,128)}, f32[640,2048]{1,0:T(8,128)}) custom-call(bf16[128,8,8,640]{3,2,1,0:T(8,128)(2,1)} %bitcast.4, bf16[2048,640]{1,0:T(8,128)(2,1)} %w_ref.1, s32[8,8,128]{2,1,0:T(8,128)} %reshape.20.tgt_ref), custom_call_target="tpu_custom_call" | custom-call | tf_op jit(solution)/shard_map/pallas_call | solution.py:429
  175.5 1.2 reduce_sum.9
  177.4 0.0 copy-start
  177.4 5.9 %copy.8 = f32[2048,640]{1,0:T(8,128)} copy(f32[2048,640]{0,1:T(8,128)} %bitcast.5) | data formatting | bytes 10485760
  183.3 0.0 copy-done
  183.3 0.7 copy.10
Async XLA Ops:
  177.4 5.9 %copy-start = (f32[64,640]{1,0:T(8,128)S(1)}, f32[64,640]{1,0:T(8,128)}, u32[]{:S(2)}) copy-start(f32[64,640]{1,0:T(8,128)} %get-tuple-element.19) | copy-start | bytes 491524

commit v3 on v0

v3 whole, which is shorter than its diff:
```python
import functools

import jax
import jax.numpy as jnp
from jax import lax
from jax.experimental import pallas as pl
from jax.experimental.pallas import tpu as pltpu
from jax.sharding import PartitionSpec as P

MESH = pl.DeviceIdType.MESH
F32 = jnp.float32
BF16 = jnp.bfloat16
COMM = True

TOKENS, DIM, VOCAB = 8192, 640, 2048
UNITS, ROWS = 8, 8
SIZE = TOKENS // UNITS
BLOCK = 256
FEW = 16
SLOTS = 4
LANES = ((0, 256), (256, 512), (512, 640))
STRIDES = (2, 8, 32)


def mod(a, n):
    return a % n if isinstance(a, int) else lax.rem(a, jnp.int32(n))


def div(a, n):
    return a // n if isinstance(a, int) else lax.div(a, jnp.int32(n))


def dot(a, b, ca, cb):
    return lax.dot_general(a, b, (((ca,), (cb,)), ((), ())), preferred_element_type=F32)


def pick(n, values):
    return jnp.where(n == 0, values[0], jnp.where(n == 1, values[1], values[2]))


def remote(src, dst, send, recv, dev):
    return pltpu.make_async_remote_copy(
        src_ref=src, dst_ref=dst, send_sem=send, recv_sem=recv, device_id=(0, dev), device_id_type=MESH
    )


def merge(parts):
    top = functools.reduce(jnp.maximum, [p[0] for p in parts])
    total = functools.reduce(jnp.add, [p[1] * jnp.exp(p[0] - top) for p in parts])
    return top, total


class Place:
    def __init__(self, me):
        self.me = me
        self.g, self.q = mod(me, 8), div(me, 8)
        self.core = mod(me, 2)
        self.partner = me + 1 - 2 * self.core
        self.pos = (mod(div(me, 2), 4), mod(div(me, 8), 4), div(me, 32))
        self.row = [self.q * 8 + mod(self.g + k, 8) for k in range(1, 8)]
        self.plane = [mod(self.q + k, 16) * 8 + self.g for k in range(1, 16)]

    def along(self, axis):
        pos, stride = pick(axis, self.pos), pick(axis, STRIDES)
        at = [pos] + [mod(pos + k, 4) for k in (1, 2, 3)]
        return at, [self.me + (p - pos) * stride for p in at]

    def greet(self):
        barrier = pltpu.get_barrier_semaphore()
        for p in self.row + self.plane:
            pl.semaphore_signal(barrier, inc=1, device_id=(0, p), device_id_type=MESH)
        return barrier


class Stats:
    def __init__(self, place, bufs):
        self.p = place
        self.a, self.b, self.send, self.recv = bufs

    @staticmethod
    def scratch():
        dma = pltpu.SemaphoreType.DMA
        return [
            pltpu.VMEM((SLOTS, 8, 2, 8, 128), F32),
            pltpu.VMEM((SLOTS, 16, 2, 8, 128), F32),
            dma((SLOTS, 22)),
            dma((SLOTS, 22)),
        ]

    def first(self, t):
        s = mod(t, SLOTS)
        mine = self.a.at[s, self.p.g]
        return [remote(mine, mine, self.send.at[s, k], self.recv.at[s, k], self.p.row[k]) for k in range(7)]

    def second(self, t):
        s = mod(t, SLOTS)
        mine = self.b.at[s, self.p.q]
        return [remote(mine, mine, self.send.at[s, 7 + k], self.recv.at[s, 7 + k], self.p.plane[k]) for k in range(15)]

    def start_first(self, t):
        for c in self.first(t):
            c.start()

    def start_second(self, t):
        for c in self.first(t):
            c.wait()
        s = mod(t, SLOTS)
        self.b[s, self.p.q, 0], self.b[s, self.p.q, 1] = merge([self.a[s, k] for k in range(8)])
        for c in self.second(t):
            c.start()

    def wait_second(self, t):
        for c in self.second(t):
            c.wait()

    def lse(self, t):
        top, total = merge([self.b[mod(t, SLOTS), k] for k in range(16)])
        return top + jnp.log(total)


class Scatter:
    def __init__(self, place, bufs):
        self.p = place
        (self.pbuf, self.r0, self.s0, self.v1, self.s1, self.v2, self.s2, self.v3,
         self.csend, self.crecv, self.send, self.recv) = bufs

    @staticmethod
    def scratch():
        dma = pltpu.SemaphoreType.DMA
        widths = [b - a for a, b in LANES]
        return [
            pltpu.VMEM((64, 2, ROWS, DIM), F32),
            pltpu.VMEM((2, 64, ROWS, DIM), F32),
            [pltpu.VMEM((2, 64, ROWS, w), F32) for w in widths],
            [pltpu.VMEM((SLOTS, 6, 8, ROWS, w), F32) for w in widths],
            [pltpu.VMEM((2, 16, ROWS, w), F32) for w in widths],
            [pltpu.VMEM((SLOTS, 6, 2, ROWS, w), F32) for w in widths],
            [pltpu.VMEM((2, 4, ROWS, w), F32) for w in widths],
            [pltpu.VMEM((SLOTS, 3, ROWS, w), F32) for w in widths],
            dma((2,)), dma((2,)), dma((SLOTS, 3, 15)), dma((SLOTS, 3, 15)),
        ]

    def line(self, u, j, level):
        return self.p.along(mod(u + j + level, 3))

    def bufs(self, level):
        return ((self.s0, self.v1), (self.s1, self.v2))[level]

    def piece(self, level, half, owner):
        n = (8, 2)[level]
        return pl.ds((half * 4 + owner) * n, n)

    def core_copy(self, u):
        s = mod(u, 2)
        return remote(self.pbuf.at[:, 1 - self.p.core], self.r0.at[s], self.csend.at[s], self.crecv.at[s], self.p.partner)

    def ring_copies(self, u, j, level, kinds, line):
        src, dst = self.bufs(level)
        at, dev = line
        s, v = mod(u, 2), mod(u, SLOTS)
        copies = []
        for kind in kinds:
            half, step, way = ((0, 2, 1), (1, 2, 3), (1, 1, 1), (0, 3, 3), (0, 1, 1), (1, 3, 3))[kind]
            n = level * 6 + kind
            copies.append(remote(
                src[j].at[s, self.piece(level, half, at[step])], dst[j].at[v, kind], self.send.at[v, j, n],
                self.recv.at[v, j, n], dev[way],
            ))
        return copies

    def last_copies(self, u, j, line):
        at, dev = line
        s, v = mod(u, 2), mod(u, SLOTS)
        return [
            remote(self.s2[j].at[s, at[k]], self.v3[j].at[v, k - 1], self.send.at[v, j, 11 + k], self.recv.at[v, j, 11 + k], dev[k])
            for k in (1, 2, 3)
        ]

    def start_core(self, u):
        self.core_copy(u).start()

    def spread(self, u):
        c = self.core_copy(u)
        c.wait_recv()
        s = mod(u, 2)
        roles = [[mod(n + 3 * UNITS - u - j, 3) for n in range(3)] for j in range(3)]
        at = [[[pick(roles[j][n], (8 * v, 2 * v, v // 2 * 32 + v % 2)) for v in range(4)] for n in range(2)] for j in range(3)]

        def body(z, _):
            last = (8 * z, 2 * z, div(z, 2) * 32 + mod(z, 2))
            for j, (lo, hi) in enumerate(LANES):
                base = pick(roles[j][2], last)
                for i in range(16):
                    n = base + (at[j][0][i % 4] + at[j][1][i // 4])
                    self.s0[j][s, n] = self.pbuf[z * 16 + i, self.p.core, :, lo:hi] + self.r0[s, z * 16 + i, :, lo:hi]
            return 0

        lax.fori_loop(0, 4, body, 0)
        for j in range(3):
            for copy in self.ring_copies(u, j, 0, range(4), self.line(u, j, 0)):
                copy.start()
        c.wait_send()

    def relay(self, u, level):
        src, dst = self.bufs(level)
        s, v = mod(u, 2), mod(u, SLOTS)
        for j in range(3):
            line = self.line(u, j, level)
            far = self.ring_copies(u, j, level, range(2), line)
            on = self.ring_copies(u, j, level, range(4, 6), line)
            for kind in range(2):
                blocks = self.piece(level, kind, line[0][(1, 3)[kind]])
                far[kind].wait_recv()
                src[j][s, blocks] = src[j][s, blocks] + dst[j][v, kind]
                on[kind].start()

    def settle(self, u, level):
        src, dst = self.bufs(level)
        s, v = mod(u, 2), mod(u, SLOTS)
        sent = []
        for j in range(3):
            line = self.line(u, j, level)
            copies = self.ring_copies(u, j, level, range(6), line)
            sent += copies
            for copy in copies[2:]:
                copy.wait_recv()
            for half in range(2):
                total = (src[j][s, self.piece(level, half, line[0][0])] + dst[j][v, 4 + half]) + dst[j][v, 3 - half]
                if level == 0:
                    self.s1[j][s, half * 8 : half * 8 + 8] = total
                else:
                    self.s2[j][s, half * 2 : half * 2 + 2] = total
            after = self.line(u, j, level + 1)
            for copy in self.last_copies(u, j, after) if level else self.ring_copies(u, j, 1, range(4), after):
                copy.start()
        for copy in sent:
            copy.wait_send()

    def finish(self, u, out_ref):
        s, v = mod(u, 2), mod(u, SLOTS)
        for j, (lo, hi) in enumerate(LANES):
            line = self.line(u, j, 2)
            copies = self.last_copies(u, j, line)
            for copy in copies:
                copy.wait_recv()
            total = (self.s2[j][s, line[0][0]] + self.v3[j][v, 0]) + (self.v3[j][v, 1] + self.v3[j][v, 2])
            out_ref[pl.ds(pl.multiple_of(u * ROWS, ROWS), ROWS), lo:hi] = total
            for copy in copies:
                copy.wait_send()


def main_kernel(h_ref, w_ref, tgt_ref, loss_ref, dh_ref, dw_ref, hb, wb, zb, dzb, acc, lse_col, tgt_col, lost,
                la, lb, h_sem, w_sem, out_sem, lsend, lrecv, *bufs):
    place = Place(lax.axis_index("fsdp") if COMM else jnp.minimum(tgt_ref[0, 0, 0], 0) + 5)
    stats = Stats(place, bufs[:4])
    rs = Scatter(place, bufs[4:])
    start = place.me * VOCAB
    blocks, quarter = SIZE // BLOCK, VOCAB // 4

    def load_h(t):
        return pltpu.make_async_copy(h_ref.at[:, t], hb.at[mod(t, 4)], h_sem.at[mod(t, 4)])

    load_w = pltpu.make_async_copy(w_ref, wb, w_sem)
    load_w.start()
    load_h(0).start()
    if COMM:
        barrier = place.greet()
    acc[...] = jnp.zeros_like(acc)
    lost[...] = jnp.zeros_like(lost)
    load_w.wait()

    lane = lax.broadcasted_iota(jnp.int32, (FEW, 128), 1)
    column = lax.broadcasted_iota(jnp.int32, (FEW, VOCAB), 1)

    def wide(x):
        return jnp.concatenate([x] * (VOCAB // 128), axis=1)

    def logits(t, rb):
        d = BLOCK // ROWS
        h = hb[mod(t, 4), rb * d : (rb + 1) * d].reshape(BLOCK, DIM)
        zb[mod(t, 3), rb * BLOCK : (rb + 1) * BLOCK, :] = dot(h, wb[...], 1, 1)

    def local_stats(t, n):
        z, s = mod(t, 3), mod(t, SLOTS)
        cols = []
        for r in range(n * 128, n * 128 + 128, FEW):
            x = zb[z, r : r + FEW, :]
            top = jnp.max(x, axis=1, keepdims=True)
            total = jnp.sum(jnp.exp(x - top), axis=1, keepdims=True)
            cols.append(jnp.where(lane == 0, top, total))
        packed = jnp.concatenate(cols, axis=0).T
        for i in range(2):
            stats.a[s, place.g, i, n : n + 1] = packed[i : i + 1]

    def columns(u):
        lse = stats.lse(u)
        for g in range(8):
            rows = slice(g * 128, (g + 1) * 128)
            lse_col[rows, :] = jnp.broadcast_to(lse[g : g + 1], (128, 128)).T
            tgt_col[rows, :] = jnp.broadcast_to(tgt_ref[u, g : g + 1, :] - start, (128, 128)).T

    def grad_logits(u, first, last):
        for r in range(first * 64, last * 64, FEW):
            rows = slice(r, r + FEW)
            x = zb[mod(u, 3), rows, :] - wide(lse_col[rows, :])
            hit = column == wide(tgt_col[rows, :])
            dzb[rows, :] = ((jnp.exp(x) - jnp.where(hit, 1.0, 0.0)) * (1.0 / TOKENS)).astype(BF16)
            found = jnp.where(hit, x, 0.0)
            lost[...] += sum(found[:, c : c + 128] for c in range(0, VOCAB, 128))

    def grad_hidden(rb):
        d = BLOCK // ROWS // 2
        rows = slice(rb * BLOCK, (rb + 1) * BLOCK)
        rs.pbuf[rb * d : (rb + 1) * d] = dot(dzb[rows, :], wb[...], 1, 0).reshape(d, 2, ROWS, DIM)

    def grad_weight(u):
        for lo in range(0, VOCAB, quarter):
            acc[:, lo : lo + quarter] += dot(hb[mod(u, 4)].reshape(SIZE, DIM), dzb[:, lo : lo + quarter], 0, 0)

    def when(cond, f, *args):
        if COMM:
            pl.when(cond)(lambda: f(*args))

    def step(t, _):
        u, old, older = t - 2, t - 3, t - 4
        mix = (t >= 3) & (t < UNITS)
        ending = t >= UNITS
        alone = (t >= 2) & ((t - 3) * (UNITS - 1 - t) < 0)

        @pl.when(t + 1 < UNITS)
        def _():
            load_h(t + 1).start()

        @pl.when(t < UNITS)
        def _():
            load_h(t).wait()

        for rb in range(blocks + 1):
            @pl.when(t < 3)
            def first():
                if rb < blocks:
                    logits(t, rb)
                if rb:
                    local_stats(t, 2 * rb - 2)
                    local_stats(t, 2 * rb - 1)

        if COMM:
            when(t < 3, stats.start_first, t)
            when((t >= 1) & (t < 3), stats.start_second, t - 1)
            when(t >= 2, stats.wait_second, u)
            when(t == UNITS + 1, rs.relay, older, 1)

        @pl.when(mix)
        def mixed_logits():
            logits(t, 0)
            columns(u)
            grad_logits(u, 0, 4)
            for rb in range(1, blocks):
                logits(t, rb)
                local_stats(t, 2 * rb - 2)
                local_stats(t, 2 * rb - 1)
                grad_logits(u, 3 + rb, 4 + rb)

        when(mix & (old >= 0), rs.relay, old, 0)
        when(mix & (older >= 0), rs.settle, older, 1)

        @pl.when(mix)
        def mixed_hidden():
            grad_hidden(0)
            local_stats(t, 6)
            local_stats(t, 7)
            grad_logits(u, 7, 8)

        when(mix, stats.start_first, t)

        @pl.when(alone)
        def alone_logits():
            columns(u)
            grad_logits(u, 0, 4)

        @pl.when(alone)
        def alone_hidden():
            grad_hidden(0)
            grad_logits(u, 4, 8)

        @pl.when(t >= 2)
        def hidden():
            grad_hidden(1)
            grad_logits(u, 8, 12)
            grad_hidden(2)
            grad_logits(u, 12, 16)
            grad_hidden(3)

        when(t >= 2, rs.start_core, u)
        when(ending, rs.relay, old, 0)
        when(ending, rs.settle, older, 1)
        when(mix & (old >= 0), rs.settle, old, 0)
        when(mix & (older >= 0), rs.finish, older, dh_ref)
        pl.when(t >= 2)(lambda: grad_weight(u))
        when(mix & (old >= 0), rs.relay, old, 1)
        when(ending, rs.settle, old, 0)
        when(ending, rs.finish, older, dh_ref)
        when(t >= 2, rs.spread, u)
        when((t >= 2) & (t < UNITS), stats.start_second, t)
        return 0

    if COMM:
        pl.semaphore_wait(barrier, 22)
    lax.fori_loop(0, UNITS + 2, step, 0)

    def to_rows(n):
        z, r = n // 2, n % 2 * quarter
        for i in range(0, quarter, 128):
            zb[z, r + i : r + i + 128, 0:DIM] = acc[:, n * quarter + i : n * quarter + i + 128].T
        put(n).start()

    def put(n):
        z, r = n // 2, n % 2 * quarter
        return pltpu.make_async_copy(
            zb.at[z, pl.ds(r, quarter), pl.ds(0, DIM)], dw_ref.at[pl.ds(n * quarter, quarter)], out_sem.at[n]
        )

    mine = jnp.sum(lost[...], axis=0, keepdims=True)
    if not COMM:
        for n in range(4):
            to_rows(n)
        loss_ref[...] = jnp.sum(mine, axis=1, keepdims=True)
        for n in range(4):
            put(n).wait()
        return
    la[place.g] = mine
    row = [remote(la.at[place.g], la.at[place.g], lsend.at[k], lrecv.at[k], place.row[k]) for k in range(7)]
    plane = [remote(lb.at[place.q], lb.at[place.q], lsend.at[7 + k], lrecv.at[7 + k], place.plane[k]) for k in range(15)]
    for c in row:
        c.start()
    rs.relay(6, 1)
    to_rows(0)
    to_rows(1)
    rs.relay(7, 0)
    to_rows(2)
    for c in row:
        c.wait()
    lb[place.q] = functools.reduce(jnp.add, [la[k] for k in range(8)])
    for c in plane:
        c.start()
    to_rows(3)
    rs.settle(7, 0)
    rs.settle(6, 1)
    rs.relay(7, 1)
    rs.finish(6, dh_ref)
    rs.settle(7, 1)
    for c in plane:
        c.wait()
    total = functools.reduce(jnp.add, [lb[k] for k in range(16)])
    loss_ref[...] = jnp.sum(total, axis=1, keepdims=True) * (-1.0 / TOKENS)
    rs.finish(7, dh_ref)
    for n in range(4):
        put(n).wait()


def fused(hidden, targets, w_blk):
    dma = pltpu.SemaphoreType.DMA
    any_spec, vmem = pl.BlockSpec(memory_space=pl.ANY), pl.BlockSpec(memory_space=pltpu.VMEM)
    return pl.pallas_call(
        main_kernel,
        out_shape=(
            jax.ShapeDtypeStruct((1, 1), F32),
            jax.ShapeDtypeStruct((64, DIM), F32),
            jax.ShapeDtypeStruct((VOCAB, DIM), F32),
        ),
        in_specs=[any_spec, any_spec, vmem],
        out_specs=(vmem, vmem, any_spec),
        scratch_shapes=[
            pltpu.VMEM((4, 128, ROWS, DIM), BF16),
            pltpu.VMEM((VOCAB, DIM), BF16),
            pltpu.VMEM((3, SIZE, VOCAB), F32),
            pltpu.VMEM((SIZE, VOCAB), BF16),
            pltpu.VMEM((DIM, VOCAB), F32),
            pltpu.VMEM((SIZE, 128), F32),
            pltpu.VMEM((SIZE, 128), jnp.int32),
            pltpu.VMEM((FEW, 128), F32),
            pltpu.VMEM((8, 1, 128), F32),
            pltpu.VMEM((16, 1, 128), F32),
            dma((4,)), dma, dma((4,)), dma((22,)), dma((22,)),
        ] + Stats.scratch() + Scatter.scratch(),
        compiler_params=pltpu.CompilerParams(
            vmem_limit_bytes=67043328, **(dict(collective_id=0, has_side_effects=True) if COMM else {})
        ),
    )(hidden, w_blk, targets)


def prepare(hidden, targets):
    h = hidden.reshape(128, UNITS, ROWS, DIM)
    t = targets.reshape(128, UNITS, ROWS).transpose(1, 0, 2).reshape(UNITS, 8, 128)
    return h, t


def solution(mesh):
    def local_step(hidden, targets, w_blk):
        h, t = prepare(hidden, targets)
        loss, grad_hid, grad_w = fused(h, t, w_blk)
        return loss.reshape(1), grad_hid, grad_w

    return jax.shard_map(
        local_step,
        mesh=mesh,
        in_specs=(P("data", None), P("data"), P("fsdp", None)),
        out_specs=(P("data"), P(("data", "fsdp"), None), P(("data", "fsdp"), None)),
        check_vma=False,
    )
```

time: 1030 us -> 158 us (0.15)
  waiting for transfers between devices: 785 us -> 0 us
  Pallas kernels: 0 us -> 146 us
  matrix products: 103 us -> 0 us
  blocking collectives: 68.3 us -> 0 us
  other arithmetic: 57.1 us -> 0 us
  between operations: 15.9 us -> 2.46 us
    reduce_scatter x1 -> x0, waiting for transfers between devices: 644 us -> none  [local_step(): lax.psum_scatter(grad_part, 'fsdp', scatter_dimension=0, tiled=True)]
    pallas_call x0 -> x1, Pallas kernels: none -> 146 us  [fused(): pl.pallas_call(main_kernel, out_shape=(jax.ShapeDtypeStruct((1, 1), F32),...]
    psum x1 -> x0, waiting for transfers between devices: 141 us -> none  [local_step(): group_stats = lax.psum(jnp.concatenate([exp_sum, tgt_part], axis=1), 'fsdp')]
    dot_general x3 -> x0, matrix products: 103 us -> none  [the longest x1 35.5 us: local_step(): jnp.einsum('td,vd->tv', hidden, w_blk, preferred_element_type=jnp.float32)]
    pmax x1 -> x0, blocking collectives: 68.3 us -> none  [local_step(): row_max = lax.pmax(jnp.max(logits, axis=1, keepdims=True), 'fsdp')]
    convert_element_type x1 -> x0, other arithmetic: 33.3 us -> none  [local_step(): ((jnp.exp(logits - log_norm) - tgt_hit.astype(jnp.float32)) / tok_group)....]
    reduce_sum x2 -> x0, other arithmetic: 23.1 us -> none  [the longest x1 21.5 us: local_step(): exp_sum = jnp.sum(jnp.exp(logits - row_max), axis=1, keepdims=True)]
  transfers between devices with their start and end apart: 2 -> 0, of which waited for: 2 -> 0; matrix products, arithmetic and copies ran while one was open for 3% -> 0% of each run, Pallas kernels for 0% -> 0%
where the time goes in v3:
time: 158 us
  Pallas kernels  146 us (92%)
  local copies, waits for them, and re-layouts  8.77 us (6%)
  between operations  2.46 us (2%)
    pallas_call x1, Pallas kernels, fused(): pl.pallas_call(main_kernel, out_shape=(jax.ShapeDtypeStruct((1, 1), F32),...  146 us
    unnamed x2, local copies, waits for them, and re-layouts  6.77 us

profile of v3, /device:TPU:0, one launch (start us, length us, event | category | flops | bytes accessed | tf_op | source)
XLA Modules:
  0.0 157.6 jit_solution(3296471093902696110)
XLA Ops:
  0.6 1.0 reshape.19
  1.7 0.1 copy.6
  1.8 0.8 reshape.20.tgt_ref
  2.6 146.3 %shard_map.58 = (f32[1,1]{1,0:T(1,128)}, f32[64,640]{1,0:T(8,128)}, f32[2048,640]{1,0:T(8,128)}) custom-call(bf16[128,8,8,640]{3,2,1,0:T(8,128)(2,1)} %bitcast.3, bf16[2048,640]{1,0:T(8,128)(2,1)} %w_ref.1, s32[8,8,128]{2,1,0:T(8,128)} %reshape.20.tgt_ref), custom_call_target="tpu_custom_call" | custom-call | tf_op jit(solution)/shard_map/pallas_call | solution.py:464
  149.7 1.6 %copy.11 = f32[64,640]{1,0:T(8,128)} copy(f32[64,640]{1,0:T(8,128)} %get-tuple-element.13) | data formatting | bytes 327680
  151.2 5.2 %copy.12 = f32[2048,640]{1,0:T(8,128)} copy(f32[2048,640]{1,0:T(8,128)} %get-tuple-element.14) | data formatting | bytes 10485760

commit v4 on v3

--- a/solution.py
+++ b/solution.py
@@ -313,9 +313,9 @@
         rows = slice(rb * BLOCK, (rb + 1) * BLOCK)
         rs.pbuf[rb * d : (rb + 1) * d] = dot(dzb[rows, :], wb[...], 1, 0).reshape(d, 2, ROWS, DIM)
 
-    def grad_weight(u):
-        for lo in range(0, VOCAB, quarter):
-            acc[:, lo : lo + quarter] += dot(hb[mod(u, 4)].reshape(SIZE, DIM), dzb[:, lo : lo + quarter], 0, 0)
+    def weight_block(u, n):
+        cols = slice(n * quarter, (n + 1) * quarter)
+        acc[:, cols] += dot(hb[mod(u, 4)].reshape(SIZE, DIM), dzb[:, cols], 0, 0)
 
     def when(cond, f, *args):
         if COMM:
@@ -323,89 +323,66 @@
 
     def step(t, _):
         u, old, older = t - 2, t - 3, t - 4
-        mix = (t >= 3) & (t < UNITS)
+        early = t < UNITS
         ending = t >= UNITS
-        alone = (t >= 2) & ((t - 3) * (UNITS - 1 - t) < 0)
 
         @pl.when(t + 1 < UNITS)
         def _():
             load_h(t + 1).start()
 
-        @pl.when(t < UNITS)
+        @pl.when(early)
         def _():
             load_h(t).wait()
 
-        for rb in range(blocks + 1):
-            @pl.when(t < 3)
-            def first():
-                if rb < blocks:
-                    logits(t, rb)
+        @pl.when(early)
+        def logits_and_stats():
+            for rb in range(blocks):
+                logits(t, rb)
                 if rb:
                     local_stats(t, 2 * rb - 2)
                     local_stats(t, 2 * rb - 1)
+            local_stats(t, 2 * blocks - 2)
+            local_stats(t, 2 * blocks - 1)
 
         if COMM:
-            when(t < 3, stats.start_first, t)
-            when((t >= 1) & (t < 3), stats.start_second, t - 1)
-            when(t >= 2, stats.wait_second, u)
-            when(t == UNITS + 1, rs.relay, older, 1)
-
-        @pl.when(mix)
-        def mixed_logits():
-            logits(t, 0)
+            @pl.when(t == 0)
+            def _():
+                pl.semaphore_wait(barrier, 22)
+
+        when(early, stats.start_first, t)
+        when((t >= 1) & (t < 3), stats.start_second, t - 1)
+        when(early & (old >= 0), rs.relay, old, 0)
+        when(early & (older >= 0), rs.settle, older, 1)
+        when(t >= 2, stats.wait_second, u)
+        when(t == UNITS + 1, rs.relay, older, 1)
+
+        @pl.when(t >= 2)
+        def hidden():
             columns(u)
             grad_logits(u, 0, 4)
-            for rb in range(1, blocks):
-                logits(t, rb)
-                local_stats(t, 2 * rb - 2)
-                local_stats(t, 2 * rb - 1)
-                grad_logits(u, 3 + rb, 4 + rb)
-
-        when(mix & (old >= 0), rs.relay, old, 0)
-        when(mix & (older >= 0), rs.settle, older, 1)
-
-        @pl.when(mix)
-        def mixed_hidden():
-            grad_hidden(0)
-            local_stats(t, 6)
-            local_stats(t, 7)
-            grad_logits(u, 7, 8)
-
-        when(mix, stats.start_first, t)
-
-        @pl.when(alone)
-        def alone_logits():
-            columns(u)
-            grad_logits(u, 0, 4)
-
-        @pl.when(alone)
-        def alone_hidden():
-            grad_hidden(0)
-            grad_logits(u, 4, 8)
-
-        @pl.when(t >= 2)
-        def hidden():
-            grad_hidden(1)
-            grad_logits(u, 8, 12)
-            grad_hidden(2)
-            grad_logits(u, 12, 16)
-            grad_hidden(3)
+            for rb in range(blocks):
+                grad_hidden(rb)
+                if rb + 1 < blocks:
+                    grad_logits(u, 4 * rb + 4, 4 * rb + 8)
 
         when(t >= 2, rs.start_core, u)
         when(ending, rs.relay, old, 0)
         when(ending, rs.settle, older, 1)
-        when(mix & (old >= 0), rs.settle, old, 0)
-        when(mix & (older >= 0), rs.finish, older, dh_ref)
-        pl.when(t >= 2)(lambda: grad_weight(u))
-        when(mix & (old >= 0), rs.relay, old, 1)
-        when(ending, rs.settle, old, 0)
-        when(ending, rs.finish, older, dh_ref)
-        when(t >= 2, rs.spread, u)
-        when((t >= 2) & (t < UNITS), stats.start_second, t)
+        when(early & (old >= 0), rs.settle, old, 0)
+        when(early & (older >= 0), rs.finish, older, dh_ref)
+
+        @pl.when((t >= 2) & (t < UNITS + 1))
+        def weight():
+            for n in range(4):
+                weight_block(u, n)
+
+        when(early & (old >= 0), rs.relay, old, 1)
+        when(t == UNITS, rs.settle, old, 0)
+        when(t == UNITS, rs.finish, older, dh_ref)
+        when((t >= 2) & (t < UNITS + 1), rs.spread, u)
+        when((t >= 2) & early, stats.start_second, t)
         return 0
 
-    if COMM:
-        pl.semaphore_wait(barrier, 22)
     lax.fori_loop(0, UNITS + 2, step, 0)
 
     def to_rows(n):
@@ -423,6 +400,7 @@
     mine = jnp.sum(lost[...], axis=0, keepdims=True)
     if not COMM:
         for n in range(4):
+            weight_block(7, n)
             to_rows(n)
         loss_ref[...] = jnp.sum(mine, axis=1, keepdims=True)
         for n in range(4):
@@ -433,21 +411,28 @@
     plane = [remote(lb.at[place.q], lb.at[place.q], lsend.at[7 + k], lrecv.at[7 + k], place.plane[k]) for k in range(15)]
     for c in row:
         c.start()
+    weight_block(7, 0)
+    rs.settle(6, 0)
+    rs.finish(5, dh_ref)
+    weight_block(7, 1)
+    rs.spread(7)
+    weight_block(7, 2)
+    to_rows(0)
     rs.relay(6, 1)
-    to_rows(0)
+    rs.relay(7, 0)
+    weight_block(7, 3)
     to_rows(1)
-    rs.relay(7, 0)
-    to_rows(2)
     for c in row:
         c.wait()
     lb[place.q] = functools.reduce(jnp.add, [la[k] for k in range(8)])
     for c in plane:
         c.start()
-    to_rows(3)
     rs.settle(7, 0)
     rs.settle(6, 1)
+    to_rows(2)
     rs.relay(7, 1)
     rs.finish(6, dh_ref)
+    to_rows(3)
     rs.settle(7, 1)
     for c in plane:
         c.wait()

time: 158 us -> 152 us (0.962)
  Pallas kernels: 146 us -> 140 us
    pallas_call x1, Pallas kernels: 146 us -> 140 us  [fused(): pl.pallas_call(main_kernel, out_shape=(jax.ShapeDtypeStruct((1, 1), F32),...]
where the time goes in v4:
time: 152 us; the launch traced here: 151 us
  Pallas kernels  140 us (92%)
  local copies, waits for them, and re-layouts  8.77 us (6%)
  between operations  2.46 us (2%)
    pallas_call x1, Pallas kernels, fused(): pl.pallas_call(main_kernel, out_shape=(jax.ShapeDtypeStruct((1, 1), F32),...  140 us
    unnamed x2, local copies, waits for them, and re-layouts  6.77 us

profile of v4, /device:TPU:0, one launch (start us, length us, event | category | flops | bytes accessed | tf_op | source)
XLA Modules:
  0.0 151.3 jit_solution(12399469797843307386)
XLA Ops:
  0.6 1.0 reshape.19
  1.7 0.1 copy.6
  1.8 0.8 reshape.20.tgt_ref
  2.6 140.0 %shard_map.58 = (f32[1,1]{1,0:T(1,128)}, f32[64,640]{1,0:T(8,128)}, f32[2048,640]{1,0:T(8,128)}) custom-call(bf16[128,8,8,640]{3,2,1,0:T(8,128)(2,1)} %bitcast.3, bf16[2048,640]{1,0:T(8,128)(2,1)} %w_ref.1, s32[8,8,128]{2,1,0:T(8,128)} %reshape.20.tgt_ref), custom_call_target="tpu_custom_call" | custom-call | tf_op jit(solution)/shard_map/pallas_call | solution.py:449
  143.4 1.6 %copy.11 = f32[64,640]{1,0:T(8,128)} copy(f32[64,640]{1,0:T(8,128)} %get-tuple-element.13) | data formatting | bytes 327680
  145.0 5.2 %copy.12 = f32[2048,640]{1,0:T(8,128)} copy(f32[2048,640]{1,0:T(8,128)} %get-tuple-element.14) | data formatting | bytes 10485760

commit v5 on v4

--- a/solution.py
+++ b/solution.py
@@ -17,6 +17,7 @@
 SIZE = TOKENS // UNITS
 BLOCK = 256
 FEW = 16
+PIECES = 8
 SLOTS = 4
 LANES = ((0, 256), (256, 512), (512, 640))
 STRIDES = (2, 8, 32)
@@ -304,18 +305,18 @@
             rows = slice(r, r + FEW)
             x = zb[mod(u, 3), rows, :] - wide(lse_col[rows, :])
             hit = column == wide(tgt_col[rows, :])
-            dzb[rows, :] = ((jnp.exp(x) - jnp.where(hit, 1.0, 0.0)) * (1.0 / TOKENS)).astype(BF16)
+            dzb[mod(u, 2), rows, :] = ((jnp.exp(x) - jnp.where(hit, 1.0, 0.0)) * (1.0 / TOKENS)).astype(BF16)
             found = jnp.where(hit, x, 0.0)
             lost[...] += sum(found[:, c : c + 128] for c in range(0, VOCAB, 128))
 
-    def grad_hidden(rb):
+    def grad_hidden(u, rb):
         d = BLOCK // ROWS // 2
         rows = slice(rb * BLOCK, (rb + 1) * BLOCK)
-        rs.pbuf[rb * d : (rb + 1) * d] = dot(dzb[rows, :], wb[...], 1, 0).reshape(d, 2, ROWS, DIM)
+        rs.pbuf[rb * d : (rb + 1) * d] = dot(dzb[mod(u, 2), rows, :], wb[...], 1, 0).reshape(d, 2, ROWS, DIM)
 
     def weight_block(u, n):
         cols = slice(n * quarter, (n + 1) * quarter)
-        acc[:, cols] += dot(hb[mod(u, 4)].reshape(SIZE, DIM), dzb[:, cols], 0, 0)
+        acc[:, cols] += dot(hb[mod(u, 4)].reshape(SIZE, DIM), dzb[mod(u, 2), :, cols], 0, 0)
 
     def when(cond, f, *args):
         if COMM:
@@ -325,10 +326,6 @@
         u, old, older = t - 2, t - 3, t - 4
         early = t < UNITS
         ending = t >= UNITS
-
-        @pl.when(t + 1 < UNITS)
-        def _():
-            load_h(t + 1).start()
 
         @pl.when(early)
         def _():
@@ -349,37 +346,39 @@
             def _():
                 pl.semaphore_wait(barrier, 22)
 
+        when(old >= 0, rs.spread, old)
         when(early, stats.start_first, t)
         when((t >= 1) & (t < 3), stats.start_second, t - 1)
-        when(early & (old >= 0), rs.relay, old, 0)
-        when(early & (older >= 0), rs.settle, older, 1)
+        when(early & (older >= 0), rs.relay, older, 1)
+        when(t == UNITS + 1, rs.finish, UNITS - 4, dh_ref)
         when(t >= 2, stats.wait_second, u)
-        when(t == UNITS + 1, rs.relay, older, 1)
 
         @pl.when(t >= 2)
         def hidden():
             columns(u)
             grad_logits(u, 0, 4)
             for rb in range(blocks):
-                grad_hidden(rb)
+                grad_hidden(u, rb)
                 if rb + 1 < blocks:
                     grad_logits(u, 4 * rb + 4, 4 * rb + 8)
 
         when(t >= 2, rs.start_core, u)
-        when(ending, rs.relay, old, 0)
-        when(ending, rs.settle, older, 1)
-        when(early & (old >= 0), rs.settle, old, 0)
-        when(early & (older >= 0), rs.finish, older, dh_ref)
-
-        @pl.when((t >= 2) & (t < UNITS + 1))
+        when(old >= 0, rs.relay, old, 0)
+        when(ending, rs.relay, older, 1)
+        when(early & (older >= 0), rs.settle, older, 1)
+
+        @pl.when(old >= 0)
         def weight():
             for n in range(4):
-                weight_block(u, n)
-
-        when(early & (old >= 0), rs.relay, old, 1)
-        when(t == UNITS, rs.settle, old, 0)
-        when(t == UNITS, rs.finish, older, dh_ref)
-        when((t >= 2) & (t < UNITS + 1), rs.spread, u)
+                weight_block(old, n)
+
+        @pl.when(t + 1 < UNITS)
+        def _():
+            load_h(t + 1).start()
+
+        when(old >= 0, rs.settle, old, 0)
+        when(ending, rs.settle, older, 1)
+        when((t < UNITS) & (older >= 0), rs.finish, older, dh_ref)
         when((t >= 2) & early, stats.start_second, t)
         return 0
 
@@ -412,16 +411,13 @@
     for c in row:
         c.start()
     weight_block(7, 0)
-    rs.settle(6, 0)
+    rs.spread(7)
     rs.finish(5, dh_ref)
     weight_block(7, 1)
-    rs.spread(7)
+    rs.relay(7, 0)
+    rs.relay(6, 1)
     weight_block(7, 2)
     to_rows(0)
-    rs.relay(6, 1)
-    rs.relay(7, 0)
-    weight_block(7, 3)
-    to_rows(1)
     for c in row:
         c.wait()
     lb[place.q] = functools.reduce(jnp.add, [la[k] for k in range(8)])
@@ -429,9 +425,11 @@
         c.start()
     rs.settle(7, 0)
     rs.settle(6, 1)
-    to_rows(2)
+    weight_block(7, 3)
+    to_rows(1)
     rs.relay(7, 1)
     rs.finish(6, dh_ref)
+    to_rows(2)
     to_rows(3)
     rs.settle(7, 1)
     for c in plane:
@@ -459,7 +457,7 @@
             pltpu.VMEM((4, 128, ROWS, DIM), BF16),
             pltpu.VMEM((VOCAB, DIM), BF16),
             pltpu.VMEM((3, SIZE, VOCAB), F32),
-            pltpu.VMEM((SIZE, VOCAB), BF16),
+            pltpu.VMEM((2, SIZE, VOCAB), BF16),
             pltpu.VMEM((DIM, VOCAB), F32),
             pltpu.VMEM((SIZE, 128), F32),
             pltpu.VMEM((SIZE, 128), jnp.int32),
@@ -474,6 +472,34 @@
     )(hidden, w_blk, targets)
 
 
+def deliver_kernel(loss_in, dh_in, dw_in, loss_out, dh_out, dw_out, buf, load, store):
+    rows = VOCAB // PIECES
+    at = [pl.ds(n * rows, rows) for n in range(PIECES)]
+    loads = [pltpu.make_async_copy(dw_in.at[a], buf.at[a], load.at[n]) for n, a in enumerate(at)]
+    stores = [pltpu.make_async_copy(buf.at[a], dw_out.at[a], store.at[n]) for n, a in enumerate(at)]
+    for copy in loads:
+        copy.start()
+    loss_out[...] = loss_in[...]
+    dh_out[...] = dh_in[...]
+    for one, other in zip(loads, stores):
+        one.wait()
+        other.start()
+    for copy in stores:
+        copy.wait()
+
+
+def deliver(loss, grad_hid, grad_w):
+    any_spec, vmem = pl.BlockSpec(memory_space=pl.ANY), pl.BlockSpec(memory_space=pltpu.VMEM)
+    dma = pltpu.SemaphoreType.DMA
+    return pl.pallas_call(
+        deliver_kernel,
+        out_shape=tuple(jax.ShapeDtypeStruct(x.shape, F32) for x in (loss, grad_hid, grad_w)),
+        in_specs=[vmem, vmem, any_spec],
+        out_specs=(vmem, vmem, any_spec),
+        scratch_shapes=[pltpu.VMEM((VOCAB, DIM), F32), dma((PIECES,)), dma((PIECES,))],
+    )(loss, grad_hid, grad_w)
+
+
 def prepare(hidden, targets):
     h = hidden.reshape(128, UNITS, ROWS, DIM)
     t = targets.reshape(128, UNITS, ROWS).transpose(1, 0, 2).reshape(UNITS, 8, 128)
@@ -483,7 +509,7 @@
 def solution(mesh):
     def local_step(hidden, targets, w_blk):
         h, t = prepare(hidden, targets)
-        loss, grad_hid, grad_w = fused(h, t, w_blk)
+        loss, grad_hid, grad_w = deliver(*fused(h, t, w_blk))
         return loss.reshape(1), grad_hid, grad_w
 
     return jax.shard_map(

time: 152 us -> 157 us (1.033)
  Pallas kernels: 140 us -> 154 us
  local copies, waits for them, and re-layouts: 8.77 us -> 2 us
  between operations: 2.46 us -> 0.81 us
    pallas_call x1, Pallas kernels: 140 us -> 147 us  [fused(): pl.pallas_call(main_kernel, out_shape=(jax.ShapeDtypeStruct((1, 1), F32),...]
    pallas_call x0 -> x1, Pallas kernels: none -> 6.85 us  [deliver(): pl.pallas_call(deliver_kernel, out_shape=tuple((jax.ShapeDtypeStruct(x.sh...]
    unnamed x2 -> x0, local copies, waits for them, and re-layouts: 6.77 us -> none
where the time goes in v5:
time: 157 us
  Pallas kernels  154 us (98%)
  local copies, waits for them, and re-layouts  2 us (1%)
    pallas_call x1, Pallas kernels, fused(): pl.pallas_call(main_kernel, out_shape=(jax.ShapeDtypeStruct((1, 1), F32),...  147 us
    pallas_call x1, Pallas kernels, deliver(): pl.pallas_call(deliver_kernel, out_shape=tuple((jax.ShapeDtypeStruct(x.sh...  6.85 us

profile of v5, /device:TPU:0, one launch (start us, length us, event | category | flops | bytes accessed | tf_op | source)
XLA Modules:
  0.0 156.6 jit_solution(11825640666068420156)
XLA Ops:
  0.6 1.0 reshape.19
  1.7 0.1 copy.6
  1.8 0.8 reshape.20.tgt_ref
  2.6 146.9 %shard_map.58 = (f32[1,1]{1,0:T(1,128)}, f32[64,640]{1,0:T(8,128)}, f32[2048,640]{1,0:T(8,128)}) custom-call(bf16[128,8,8,640]{3,2,1,0:T(8,128)(2,1)} %bitcast.3, bf16[2048,640]{1,0:T(8,128)(2,1)} %w_ref.1, s32[8,8,128]{2,1,0:T(8,128)} %reshape.20.tgt_ref), custom_call_target="tpu_custom_call" | custom-call | tf_op jit(solution)/shard_map/pallas_call | solution.py:447
  149.5 6.8 %shard_map.59 = (f32[1,1]{1,0:T(1,128)}, f32[64,640]{1,0:T(8,128)}, f32[2048,640]{1,0:T(8,128)}) custom-call(f32[1,1]{1,0:T(1,128)} %get-tuple-element.9.loss_in, f32[64,640]{1,0:T(8,128)} %get-tuple-element.10.dh_in, f32[2048,640]{1,0:T(8,128)} %get-tuple-element.11.dw_in), custom_call_target="tpu_custom_call" | custom-call | tf_op jit(solution)/shard_map/pallas_call | solution.py:494

commit v6 on v4

--- a/solution.py
+++ b/solution.py
@@ -17,6 +17,7 @@
 SIZE = TOKENS // UNITS
 BLOCK = 256
 FEW = 16
+PIECES = 8
 SLOTS = 4
 LANES = ((0, 256), (256, 512), (512, 640))
 STRIDES = (2, 8, 32)
@@ -474,6 +475,33 @@
     )(hidden, w_blk, targets)
 
 
+def deliver_kernel(dh_in, dw_in, dh_out, dw_out, dh_buf, dw_buf, load, store):
+    rows = VOCAB // PIECES
+    moves = [(dw_in.at[pl.ds(n * rows, rows)], dw_buf.at[pl.ds(n * rows, rows)], dw_out.at[pl.ds(n * rows, rows)]) for n in range(PIECES)]
+    moves.append((dh_in, dh_buf, dh_out))
+    loads = [pltpu.make_async_copy(a, b, load.at[n]) for n, (a, b, _) in enumerate(moves)]
+    stores = [pltpu.make_async_copy(b, c, store.at[n]) for n, (_, b, c) in enumerate(moves)]
+    for copy in loads:
+        copy.start()
+    for one, other in zip(loads, stores):
+        one.wait()
+        other.start()
+    for copy in stores:
+        copy.wait()
+
+
+def deliver(grad_hid, grad_w):
+    any_spec, dma = pl.BlockSpec(memory_space=pl.ANY), pltpu.SemaphoreType.DMA
+    return pl.pallas_call(
+        deliver_kernel,
+        out_shape=tuple(jax.ShapeDtypeStruct(x.shape, F32) for x in (grad_hid, grad_w)),
+        in_specs=[any_spec] * 2,
+        out_specs=(any_spec,) * 2,
+        scratch_shapes=[pltpu.VMEM((64, DIM), F32), pltpu.VMEM((VOCAB, DIM), F32), dma((PIECES + 1,)), dma((PIECES + 1,))],
+        compiler_params=pltpu.CompilerParams(vmem_limit_bytes=67043328),
+    )(grad_hid, grad_w)
+
+
 def prepare(hidden, targets):
     h = hidden.reshape(128, UNITS, ROWS, DIM)
     t = targets.reshape(128, UNITS, ROWS).transpose(1, 0, 2).reshape(UNITS, 8, 128)
@@ -484,7 +512,7 @@
     def local_step(hidden, targets, w_blk):
         h, t = prepare(hidden, targets)
         loss, grad_hid, grad_w = fused(h, t, w_blk)
-        return loss.reshape(1), grad_hid, grad_w
+        return loss.reshape(1), *deliver(grad_hid, grad_w)
 
     return jax.shard_map(
         local_step,

time: 152 us -> 149 us (0.980)
  local copies, waits for them, and re-layouts: 8.77 us -> 2 us
  Pallas kernels: 140 us -> 145 us
    unnamed x2 -> x0, local copies, waits for them, and re-layouts: 6.77 us -> none
    pallas_call x0 -> x1, Pallas kernels: none -> 4.68 us  [deliver(): pl.pallas_call(deliver_kernel, out_shape=tuple((jax.ShapeDtypeStruct(x.sh...]
where the time goes in v6:
time: 149 us
  Pallas kernels  145 us (97%)
  between operations  2.42 us (2%)
  local copies, waits for them, and re-layouts  2 us (1%)
    pallas_call x1, Pallas kernels, fused(): pl.pallas_call(main_kernel, out_shape=(jax.ShapeDtypeStruct((1, 1), F32),...  140 us
    pallas_call x1, Pallas kernels, deliver(): pl.pallas_call(deliver_kernel, out_shape=tuple((jax.ShapeDtypeStruct(x.sh...  4.68 us

profile of v6, /device:TPU:0, one launch (start us, length us, event | category | flops | bytes accessed | tf_op | source)
XLA Modules:
  0.0 149.1 jit_solution(6787576715970587824)
XLA Ops:
  0.6 1.0 reshape.19
  1.7 0.1 copy.6
  1.8 0.8 reshape.20.tgt_ref
  2.6 140.0 %shard_map.58 = (f32[1,1]{1,0:T(1,128)}, f32[64,640]{1,0:T(8,128)}, f32[2048,640]{1,0:T(8,128)}) custom-call(bf16[128,8,8,640]{3,2,1,0:T(8,128)(2,1)} %bitcast.3, bf16[2048,640]{1,0:T(8,128)(2,1)} %w_ref.1, s32[8,8,128]{2,1,0:T(8,128)} %reshape.20.tgt_ref), custom_call_target="tpu_custom_call" | custom-call | tf_op jit(solution)/shard_map/pallas_call | solution.py:450
  142.7 4.7 %shard_map.59 = (f32[64,640]{1,0:T(8,128)}, f32[2048,640]{1,0:T(8,128)}) custom-call(f32[64,640]{1,0:T(8,128)} %get-tuple-element.9.dh_in, f32[2048,640]{1,0:T(8,128)} %get-tuple-element.10.dw_in), custom_call_target="tpu_custom_call" | custom-call | tf_op jit(solution)/shard_map/pallas_call | solution.py:495
